TPU v7x, 128 devices: a whole 4x4x4 slice. The times are simulated.
128 devices in a mesh: section: 16 (over z, x_hi, core), tm: 8 (over y, x_lo).
Axes of the slice: x: 4 (x_hi: 2, x_lo: 2; x = x_hi * 2 + x_lo), y: 4, z: 4, core: 2. Of those that a mesh axis runs over, the one named last changes fastest.
Arguments:
- frames: bfloat16 [4, 512, 1024], P(None, 'tm'), may hold values from -6 to 6, as said below
- lengths: int32 [4], replicated, may hold values from 128 to 512
- ffn_gain: float32 [16, 1024], P('section'), may hold values from 0.1 to 1.9
- ffn_up: bfloat16 [16, 1024, 2048], P('section'), may hold values from -0.1875 to 0.1875
- ffn_down: bfloat16 [16, 2048, 1024], P('section'), may hold values from -0.125 to 0.125
- attn_gain: float32 [16, 1024], P('section'), may hold values from 0.1 to 1.9
- query_weight: bfloat16 [16, 1024, 1024], P('section'), may hold values from -8 to 8
- key_weight: bfloat16 [16, 1024, 1024], P('section'), may hold values from -0.1875 to 0.1875
- value_weight: bfloat16 [16, 1024, 1024], P('section'), may hold values from -0.1875 to 0.1875
- out_weight: bfloat16 [16, 1024, 1024], P('section'), may hold values from -0.1875 to 0.1875
- conv_gain: float32 [16, 1024], P('section'), may hold values from 0.1 to 1.9
- expand_weight: bfloat16 [16, 1024, 2048], P('section'), may hold values from -0.1875 to 0.1875
- depth_weight: float32 [16, 31, 1024], P('section'), may hold values from -1 to 1
- depth_gain: float32 [16, 1024], P('section'), may hold values from 0.1 to 1.9
- norm_shift: float32 [16, 1024], P('section'), may hold values from -0.5 to 0.5
- shrink_weight: bfloat16 [16, 1024, 1024], P('section'), may hold values from -0.1875 to 0.1875
- final_gain: float32 [16, 1024], P('section'), may hold values from 0.1 to 1.9
Outputs:
- hidden_states: bfloat16 [16, 4, 512, 1024], P('section', None, 'tm')
Inputs may be any that keep to these rules, and one draw needn't show every extreme that they name: `frames`: input features of order one.
All inputs are finite; a program needn't handle non-finite values.
Results may differ from a plain program's by a relative error of at most 0.02.
Values may be sent and summed in bfloat16 or wider, within the bound.
A program may use at most 128 MiB of HBM per device.

v0:
```python
import math
import jax
import jax.numpy as jnp
from jax import lax
from jax.sharding import PartitionSpec as P

HEADS = 16
EPS = 1e-05


def extended(shard, sides, width):
    for axis, dim in sides:
        peers, length = (lax.axis_size(axis), shard.shape[dim])
        up = [(i, (i + 1) % peers) for i in range(peers - 1)]
        down = [(j, i) for i, j in up]
        last = lax.slice_in_dim(shard, length - width, length, axis=dim)
        initial = lax.slice_in_dim(shard, 0, width, axis=dim)
        before = lax.ppermute(last, axis, up)
        after = lax.ppermute(initial, axis, down)
        shard = jnp.concatenate([before, shard, after], axis=dim)
    return shard


def passed_along(shard, axis, by):
    peers = lax.axis_size(axis)
    pairs = [(i, i + by) for i in range(peers) if 0 <= i + by < peers]
    return lax.ppermute(shard, axis, pairs)


def normalize(value, gain):
    mean = jnp.mean(value, axis=-1, keepdims=True)
    centred = value - mean
    spread = jnp.mean(centred * centred, axis=-1, keepdims=True)
    return centred * lax.rsqrt(spread + EPS) * gain


def body(
    frames,
    lengths,
    ffn_gain,
    ffn_up,
    ffn_down,
    attn_gain,
    query_weight,
    key_weight,
    value_weight,
    out_weight,
    conv_gain,
    expand_weight,
    depth_weight,
    depth_gain,
    norm_shift,
    shrink_weight,
    final_gain,
):
    sections = lax.axis_size("section")
    groups = lax.axis_size("tm")
    section_index = lax.axis_index("section")
    group_index = lax.axis_index("tm")
    micro, rows, width = frames.shape
    whole = rows * groups
    heads = HEADS
    head = width // heads
    kernel = depth_weight.shape[1]
    rim = kernel // 2
    scale = 1.0 / math.sqrt(head)
    gain_ffn = ffn_gain[0]
    w_up = ffn_up[0]
    w_down = ffn_down[0]
    gain_a = attn_gain[0]
    w_query = query_weight[0]
    w_key = key_weight[0]
    w_value = value_weight[0]
    w_out = out_weight[0]
    gain_c = conv_gain[0]
    w_expand = expand_weight[0]
    w_depth = depth_weight[0]
    gain_depth = depth_gain[0]
    bias_depth = norm_shift[0]
    w_shrink = shrink_weight[0]
    gain_f = final_gain[0]
    local_pos = group_index * rows + jnp.arange(rows, dtype=jnp.int32)
    zero_rows = jnp.zeros((rows, width), jnp.bfloat16)
    zero_mid = jnp.zeros((rows, width), jnp.float32)

    def tick(step, carry):
        incoming, gathered = carry
        offset = step - section_index
        active = (offset >= 0) & (offset < micro)
        slot = jnp.clip(offset, 0, micro - 1)
        fresh = lax.dynamic_index_in_dim(frames, slot, 0, keepdims=False)
        inputs = jnp.where(section_index == 0, fresh, incoming)
        length = jnp.sum(jnp.where(jnp.arange(micro, dtype=jnp.int32) == slot, lengths, 0))

        def project():
            ffn_normed = normalize(inputs.astype(jnp.float32), gain_ffn).astype(jnp.bfloat16)
            inner = jax.nn.silu(
                jnp.dot(ffn_normed, w_up, preferred_element_type=jnp.float32)
            ).astype(jnp.bfloat16)
            start = inputs.astype(jnp.float32) + 0.5 * jnp.dot(
                inner, w_down, preferred_element_type=jnp.float32
            )
            normed = normalize(start, gain_a).astype(jnp.bfloat16)
            q_all, k_all, v_all = tuple(
                (
                    jnp.dot(normed, weight, preferred_element_type=jnp.float32).astype(jnp.bfloat16)
                    for weight in (w_query, w_key, w_value)
                )
            )
            return (start, q_all, k_all, v_all)

        start, queries, keys, values = lax.cond(
            active, project, lambda: (zero_mid, zero_rows, zero_rows, zero_rows)
        )
        g_query, g_key, g_value = (
            lax.all_to_all(queries, "tm", split_axis=1, concat_axis=0, tiled=True),
            lax.all_to_all(keys, "tm", split_axis=1, concat_axis=0, tiled=True),
            lax.all_to_all(values, "tm", split_axis=1, concat_axis=0, tiled=True),
        )
        local_heads = g_query.shape[1] // head
        span = 512

        def attend_groups():
            seen = jnp.arange(whole, dtype=jnp.int32) < length
            k_heads = g_key.reshape(whole, local_heads, head)
            v_heads = g_value.reshape(whole, local_heads, head)
            q_blocks = g_query.reshape(whole // span, span, local_heads, head)

            def one_block(q_block):
                scores = (
                    jnp.einsum("qgd,kgd->gqk", q_block, k_heads, preferred_element_type=jnp.float32)
                    * scale
                )
                scores = jnp.where(seen[None, None, :], scores, -1e30)
                peak = jnp.max(scores, axis=-1, keepdims=True)
                weights_h = jnp.exp(scores - peak)
                total = jnp.sum(weights_h, axis=-1, keepdims=True)
                mixed = jnp.einsum(
                    "gqk,kgd->qgd",
                    weights_h.astype(jnp.bfloat16),
                    v_heads,
                    preferred_element_type=jnp.float32,
                )
                mixed = mixed / jnp.transpose(total, (1, 0, 2))
                return mixed.astype(jnp.bfloat16).reshape(span, local_heads * head)

            return lax.map(one_block, q_blocks).reshape(whole, local_heads * head)

        grouped = lax.cond(
            active, attend_groups, lambda: jnp.zeros((whole, local_heads * head), jnp.bfloat16)
        )
        context = lax.all_to_all(grouped, "tm", split_axis=0, concat_axis=1, tiled=True)

        def conv_front():
            mid = start + jnp.dot(context, w_out, preferred_element_type=jnp.float32)
            conv_in = normalize(mid, gain_c).astype(jnp.bfloat16)
            expanded = jnp.dot(conv_in, w_expand, preferred_element_type=jnp.float32)
            keep = (local_pos < length).astype(jnp.float32)
            glu = expanded[:, :width] * jax.nn.sigmoid(expanded[:, width:]) * keep[:, None]
            return (mid, glu.astype(jnp.bfloat16))

        mid, glu = lax.cond(active, conv_front, lambda: (zero_mid, zero_rows))
        padded = extended(glu, (("tm", 0),), rim)

        def conv_back():
            widened = padded.astype(jnp.float32)
            depth = jnp.zeros((rows, width), jnp.float32)
            for offset_j in range(kernel):
                depth = depth + widened[offset_j : offset_j + rows] * w_depth[offset_j]
            shifted = normalize(depth, gain_depth) + bias_depth
            swished = (shifted * jax.nn.sigmoid(shifted)).astype(jnp.bfloat16)
            closing = mid + jnp.dot(swished, w_shrink, preferred_element_type=jnp.float32)
            return normalize(closing, gain_f).astype(jnp.bfloat16)

        result = lax.cond(active, conv_back, lambda: zero_rows)
        previous = lax.dynamic_index_in_dim(gathered, slot, 0, keepdims=False)
        gathered = lax.dynamic_update_index_in_dim(
            gathered, jnp.where(active, result, previous), slot, 0
        )
        incoming = passed_along(result, "section", 1)
        return (incoming, gathered)

    start_outs = jnp.zeros((micro, rows, width), jnp.bfloat16)
    final_in, hidden_states = lax.fori_loop(0, micro + sections - 1, tick, (zero_rows, start_outs))
    return hidden_states[None]


def solution(mesh):
    return jax.shard_map(
        body,
        mesh=mesh,
        in_specs=(
            P(None, "tm", None),
            P(),
            P("section", None),
            P("section", None, None),
            P("section", None, None),
            P("section", None),
            P("section", None, None),
            P("section", None, None),
            P("section", None, None),
            P("section", None, None),
            P("section", None),
            P("section", None, None),
            P("section", None, None),
            P("section", None),
            P("section", None),
            P("section", None, None),
            P("section", None),
        ),
        out_specs=P("section", None, "tm", None),
        check_vma=False,
    )
```

profile of v0, /device:TPU:109, one launch (start us, length us, event | category | flops | bytes accessed | tf_op | source)
XLA Modules:
  0.0 1492.9 jit_solution(9825759738350076696)
XLA Ops:
  2.5 1490.5 %while.21 = (s32[]{:T(128)}, bf16[64,1024]{1,0:T(8,128)(2,1)S(1)}, bf16[4,64,1024]{2,1,0:T(8,128)(2,1)}, s32[]{:T(128)}, s32[4]{0:T(128)}, /*index=5*/pred[]{:T(...) while((s32[]{:T(128)}, bf16[64,1024]{1,0:T(8,128)(2,1)S(1)}, ...), condition=%wide.region_22.23_spmd.clone, body=%wide.region_0.22_spmd.clone.sunk | while | flops 1626031104 | bytes 78909456 | solution.py:184
  3.3 5.0 all-to-all-start
  12.5 4.7 all-to-all-start.1
  51.9 7.7 collective-permute-done.2
  67.9 4.6 all-to-all-start.1
  107.4 12.2 collective-permute-done.2
  127.8 4.6 all-to-all-start.1
  167.2 12.2 collective-permute-done.2
  187.7 4.6 all-to-all-start.1
  227.1 12.2 collective-permute-done.2
  247.6 4.6 all-to-all-start.1
  287.0 12.2 collective-permute-done.2
  307.4 4.6 all-to-all-start.1
  346.9 12.2 collective-permute-done.2
  406.7 12.2 collective-permute-done.2
  427.2 4.6 all-to-all-start.1
  466.6 12.2 collective-permute-done.2
  487.0 4.6 all-to-all-start.1
  526.5 12.2 collective-permute-done.2
  546.9 4.6 all-to-all-start.1
  586.3 12.2 collective-permute-done.2
  606.8 4.6 all-to-all-start.1
  646.2 12.5 collective-permute-done.2
  667.1 4.6 all-to-all-start.1
  706.6 12.5 collective-permute-done.2
  727.5 4.6 all-to-all-start.1
  766.9 12.4 collective-permute-done.2
  787.6 4.6 all-to-all-start.1
  827.0 12.2 collective-permute-done.2
  847.4 4.6 all-to-all-start.1
  886.9 279.0 %collective-permute-done.2 = bf16[64,1024]{1,0:T(8,128)(2,1)S(1)} collective-permute-done((bf16[64,1024]{1,0:T(8,128)(2,1)S(1)}, bf16[64,1024]{1,0:T(8,128)(2,1)S(1)}, u32[]{:S(2)}, u32[]{:S(2)}) %collective-permute-start.2) | collective-permute-done | bytes 131104 | tf_op jit(solution)/shard_map/while/body/eval_jaxpr/ppermute | solution.py:27
  1165.8 10.7 conditional.12
  1167.1 5.2 fusion.89
  1215.0 8.2 conditional.14
  1237.5 13.3 collective-permute-done.2
  1250.8 10.7 conditional.12
  1252.1 5.2 fusion.89
  1299.9 8.2 conditional.14
  1322.4 13.3 collective-permute-done.2
  1335.7 10.7 conditional.12
  1337.0 5.2 fusion.89
  1354.6 4.6 all-to-all-start.1
  1384.8 8.2 conditional.14
  1407.3 12.8 collective-permute-done.2
  1420.1 10.7 conditional.12
  1421.4 5.2 fusion.89
  1439.0 4.6 all-to-all-start.1
  1469.2 8.2 conditional.14
  (1066 shorter events, 938.9 us)
Async XLA Ops:
  3.3 9.2 all-to-all-start
  12.5 8.9 all-to-all-start.1
  21.4 8.8 all-to-all-start.2
  49.9 9.7 collective-permute-start.2
  67.9 8.9 all-to-all-start.1
  76.8 8.8 all-to-all-start.2
  105.4 14.2 collective-permute-start.2
  127.8 8.9 all-to-all-start.1
  136.7 8.8 all-to-all-start.2
  165.2 14.2 collective-permute-start.2
  187.7 8.9 all-to-all-start.1
  196.5 8.8 all-to-all-start.2
  225.1 14.2 collective-permute-start.2
  247.6 8.9 all-to-all-start.1
  256.4 8.8 all-to-all-start.2
  285.0 14.2 collective-permute-start.2
  307.4 8.9 all-to-all-start.1
  316.3 8.8 all-to-all-start.2
  344.9 14.2 collective-permute-start.2
  367.3 8.9 all-to-all-start.1
  376.2 8.8 all-to-all-start.2
  404.7 14.2 collective-permute-start.2
  427.2 8.9 all-to-all-start.1
  436.0 8.8 all-to-all-start.2
  464.6 14.2 collective-permute-start.2
  487.0 8.9 all-to-all-start.1
  495.9 8.8 all-to-all-start.2
  524.5 14.2 collective-permute-start.2
  546.9 8.9 all-to-all-start.1
  584.4 14.2 collective-permute-start.2
  606.8 8.9 all-to-all-start.1
  644.2 14.5 collective-permute-start.2
  667.1 8.9 all-to-all-start.1
  704.6 14.5 collective-permute-start.2
  727.5 8.9 all-to-all-start.1
  764.9 14.4 collective-permute-start.2
  787.6 8.9 all-to-all-start.1
  825.0 14.2 collective-permute-start.2
  847.4 8.9 all-to-all-start.1
  884.9 280.9 %collective-permute-start.2 = (bf16[64,1024]{1,0:T(8,128)(2,1)S(1)}, bf16[64,1024]{1,0:T(8,128)(2,1)S(1)}, u32[]{:S(2)}, u32[]{:S(2)}) collective-permute-start(bf16[64,1024]{1,0:T(8,128)(2,1)S(1)} %get-tuple-element.1026), channel_id=1, source_target_pairs={{0,8},{8,16},{16,24},{24,32},{32,40},{40,48},{48,56},{56,64},{64,7... | collective-permute-start | bytes 393224 | tf_op jit(solution)/shard_map/while/body/eval_jaxpr/ppermute | solution.py:27
  1184.8 8.9 all-to-all-start.1
  1193.6 8.9 all-to-all-start.2
  1235.5 15.3 %collective-permute-start.2 = (bf16[64,1024]{1,0:T(8,128)(2,1)S(1)}, bf16[64,1024]{1,0:T(8,128)(2,1)S(1)}, u32[]{:S(2)}, u32[]{:S(2)}) collective-permute-start(bf16[64,1024]{1,0:T(8,128)(2,1)S(1)} %get-tuple-element.1026), channel_id=1, source_target_pairs={{0,8},{8,16},{16,24},{24,32},{32,40},{40,48},{48,56},{56,64},{64,7... | collective-permute-start | bytes 393224 | tf_op jit(solution)/shard_map/while/body/eval_jaxpr/ppermute | solution.py:27
  1269.7 8.9 all-to-all-start.1
  1320.4 15.3 %collective-permute-start.2 = (bf16[64,1024]{1,0:T(8,128)(2,1)S(1)}, bf16[64,1024]{1,0:T(8,128)(2,1)S(1)}, u32[]{:S(2)}, u32[]{:S(2)}) collective-permute-start(bf16[64,1024]{1,0:T(8,128)(2,1)S(1)} %get-tuple-element.1026), channel_id=1, source_target_pairs={{0,8},{8,16},{16,24},{24,32},{32,40},{40,48},{48,56},{56,64},{64,7... | collective-permute-start | bytes 393224 | tf_op jit(solution)/shard_map/while/body/eval_jaxpr/ppermute | solution.py:27
  1354.6 8.9 all-to-all-start.1
  1405.3 14.8 collective-permute-start.2
  1439.0 8.9 all-to-all-start.1
  (238 other events, 2423.1 us)
where the time goes:
time: 1500 us; the launch traced here: 1490 us
  waiting for transfers between devices  819 us (55%)
  starting transfers between devices  457 us (30%)
  local copies, waits for them, and re-layouts  89.2 us (6%)
  matrix products  70 us (5%)
  other arithmetic  52.2 us (3%)
    ppermute x19, waiting for transfers between devices, passed_along(): return lax.ppermute(shard, axis, pairs)  487 us
    all_to_all x19, starting transfers between devices, tick(): lax.all_to_all(keys, 'tm', split_axis=1, concat_axis=0, tiled=True)  88.1 us
    all_to_all x19, starting transfers between devices, tick(): lax.all_to_all(values, 'tm', split_axis=1, concat_axis=0, tiled=True)  87.8 us
    all_to_all x19, starting transfers between devices, tick(): lax.all_to_all(grouped, 'tm', split_axis=0, concat_axis=1, tiled=True)  87.8 us
    all_to_all x19, waiting for transfers between devices, tick(): lax.all_to_all(grouped, 'tm', split_axis=0, concat_axis=1, tiled=True)  80.3 us
    all_to_all x19, waiting for transfers between devices, tick(): lax.all_to_all(keys, 'tm', split_axis=1, concat_axis=0, tiled=True)  67.6 us
    ppermute x19, starting transfers between devices, extended(): after = lax.ppermute(initial, axis, down)  67.1 us
    all_to_all x19, waiting for transfers between devices, tick(): lax.all_to_all(values, 'tm', split_axis=1, concat_axis=0, tiled=True)  66.7 us
  transfers between devices with their start and end apart: 133, of which 114 were waited for; matrix products, arithmetic and copies ran while one was open for 5% of the time, Pallas kernels for 0%

commit v1 on v0

--- a/solution.py
+++ b/solution.py
@@ -149,7 +149,10 @@
         grouped = lax.cond(
             active, attend_groups, lambda: jnp.zeros((whole, local_heads * head), jnp.bfloat16)
         )
-        context = lax.all_to_all(grouped, "tm", split_axis=0, concat_axis=1, tiled=True)
+        context = jnp.concatenate(
+            lax.all_to_all(jnp.stack(jnp.split(grouped, lax.axis_size("tm"), axis=0)), "tm", 0, 0),
+            axis=1,
+        )
 
         def conv_front():
             mid = start + jnp.dot(context, w_out, preferred_element_type=jnp.float32)

time: 1500 us -> 1600 us (1.067)
  local copies, waits for them, and re-layouts: 89.2 us -> 169 us
    while x266 -> x361, local copies, waits for them, and re-layouts: 0.64 us -> 80.3 us
  transfers between devices with their start and end apart: 133 -> 133, of which waited for: 114 -> 114; matrix products, arithmetic and copies ran while one was open for 5% -> 4% of each run, Pallas kernels for 0% -> 0%
where the time goes in v1:
time: 1600 us; the launch traced here: 1580 us
  waiting for transfers between devices  833 us (52%)
  starting transfers between devices  455 us (28%)
  local copies, waits for them, and re-layouts  169 us (11%)
  matrix products  70 us (4%)
  other arithmetic  51.3 us (3%)
    ppermute x19, waiting for transfers between devices, passed_along(): return lax.ppermute(shard, axis, pairs)  499 us
    all_to_all x19, starting transfers between devices, tick(): lax.all_to_all(keys, 'tm', split_axis=1, concat_axis=0, tiled=True)  88.1 us
    all_to_all x19, starting transfers between devices, tick(): lax.all_to_all(values, 'tm', split_axis=1, concat_axis=0, tiled=True)  87.8 us
    all_to_all x19, starting transfers between devices, tick(): lax.all_to_all(jnp.stack(jnp.split(grouped, lax.axis_size('tm'), axis=0))...  87.8 us
    all_to_all x19, waiting for transfers between devices, tick(): lax.all_to_all(jnp.stack(jnp.split(grouped, lax.axis_size('tm'), axis=0))...  80.3 us
    while x361, local copies, waits for them, and re-layouts  80.3 us
    all_to_all x19, waiting for transfers between devices, tick(): lax.all_to_all(keys, 'tm', split_axis=1, concat_axis=0, tiled=True)  67.6 us
    all_to_all x19, waiting for transfers between devices, tick(): lax.all_to_all(values, 'tm', split_axis=1, concat_axis=0, tiled=True)  67.1 us
  transfers between devices with their start and end apart: 133, of which 114 were waited for; matrix products, arithmetic and copies ran while one was open for 4% of the time, Pallas kernels for 0%

profile of v1, /device:TPU:109, one launch (start us, length us, event | category | flops | bytes accessed | tf_op | source)
XLA Modules:
  0.0 1584.0 jit_solution(12952662461647068934)
XLA Ops:
  1.8 1582.2 %while.21 = (s32[]{:T(128)}, bf16[64,1024]{1,0:T(8,128)(2,1)S(1)}, bf16[4,64,1024]{2,1,0:T(8,128)(2,1)}, s32[]{:T(128)}, s32[4]{0:T(128)}, /*index=5*/pred[]{:T(...) while((s32[]{:T(128)}, bf16[64,1024]{1,0:T(8,128)(2,1)S(1)}, ...), condition=%wide.region_22.23_spmd.clone, body=%wide.region_0.22_spmd.clone.sunk | while | flops 1626031104 | bytes 78925872 | solution.py:187
  2.6 5.0 all-to-all-start
  11.8 4.7 all-to-all-start.1
  55.2 7.7 collective-permute-done.2
  71.2 4.6 all-to-all-start.1
  114.6 12.3 collective-permute-done.2
  135.2 4.6 all-to-all-start.1
  178.6 12.3 collective-permute-done.2
  199.1 4.6 all-to-all-start.1
  242.5 12.3 collective-permute-done.2
  263.1 4.6 all-to-all-start.1
  306.5 12.3 collective-permute-done.2
  327.0 4.6 all-to-all-start.1
  370.4 12.3 collective-permute-done.2
  391.0 4.6 all-to-all-start.1
  434.4 12.3 collective-permute-done.2
  498.3 12.3 collective-permute-done.2
  518.9 4.6 all-to-all-start.1
  562.3 12.3 collective-permute-done.2
  582.9 4.6 all-to-all-start.1
  626.2 12.3 collective-permute-done.2
  646.8 4.6 all-to-all-start.1
  690.2 12.3 collective-permute-done.2
  710.8 4.6 all-to-all-start.1
  754.2 12.4 collective-permute-done.2
  774.9 4.6 all-to-all-start.1
  818.4 12.4 collective-permute-done.2
  839.1 4.6 all-to-all-start.1
  882.5 12.3 collective-permute-done.2
  903.1 4.6 all-to-all-start.1
  946.5 291.1 %collective-permute-done.2 = bf16[64,1024]{1,0:T(8,128)(2,1)S(1)} collective-permute-done((bf16[64,1024]{1,0:T(8,128)(2,1)S(1)}, bf16[64,1024]{1,0:T(8,128)(2,1)S(1)}, u32[]{:S(2)}, u32[]{:S(2)}) %collective-permute-start.2) | collective-permute-done | bytes 131104 | tf_op jit(solution)/shard_map/while/body/eval_jaxpr/ppermute | solution.py:27
  1237.6 10.7 conditional.12
  1238.9 5.2 fusion.90
  1256.5 4.6 all-to-all-start.1
  1291.6 8.1 conditional.14
  1314.0 13.3 collective-permute-done.2
  1327.4 10.7 conditional.12
  1328.6 5.2 fusion.90
  1346.3 4.6 all-to-all-start.1
  1381.4 8.1 conditional.14
  1403.8 13.3 collective-permute-done.2
  1417.1 10.7 conditional.12
  1418.4 5.2 fusion.90
  1471.1 8.1 conditional.14
  1493.5 12.8 collective-permute-done.2
  1506.3 10.7 conditional.12
  1507.6 5.2 fusion.90
  1560.3 8.1 conditional.14
  (1302 shorter events, 1021.5 us)
Async XLA Ops:
  2.6 9.2 all-to-all-start
  11.8 8.9 all-to-all-start.1
  20.7 8.8 all-to-all-start.2
  53.2 9.7 collective-permute-start.2
  71.2 8.9 all-to-all-start.1
  80.1 8.8 all-to-all-start.2
  112.6 14.3 collective-permute-start.2
  135.2 8.9 all-to-all-start.1
  144.0 8.8 all-to-all-start.2
  176.6 14.3 collective-permute-start.2
  199.1 8.9 all-to-all-start.1
  208.0 8.8 all-to-all-start.2
  240.5 14.3 collective-permute-start.2
  263.1 8.9 all-to-all-start.1
  272.0 8.8 all-to-all-start.2
  304.5 14.3 collective-permute-start.2
  327.0 8.9 all-to-all-start.1
  335.9 8.8 all-to-all-start.2
  368.4 14.3 collective-permute-start.2
  391.0 8.9 all-to-all-start.1
  399.9 8.8 all-to-all-start.2
  432.4 14.3 collective-permute-start.2
  454.9 8.9 all-to-all-start.1
  463.8 8.8 all-to-all-start.2
  496.3 14.3 collective-permute-start.2
  518.9 8.9 all-to-all-start.1
  560.3 14.3 collective-permute-start.2
  582.9 8.9 all-to-all-start.1
  624.3 14.3 collective-permute-start.2
  646.8 8.9 all-to-all-start.1
  688.2 14.3 collective-permute-start.2
  710.8 8.9 all-to-all-start.1
  752.2 14.4 collective-permute-start.2
  774.9 8.9 all-to-all-start.1
  816.4 14.4 collective-permute-start.2
  839.1 8.9 all-to-all-start.1
  880.5 14.3 collective-permute-start.2
  903.1 8.9 all-to-all-start.1
  944.5 293.1 %collective-permute-start.2 = (bf16[64,1024]{1,0:T(8,128)(2,1)S(1)}, bf16[64,1024]{1,0:T(8,128)(2,1)S(1)}, u32[]{:S(2)}, u32[]{:S(2)}) collective-permute-start(bf16[64,1024]{1,0:T(8,128)(2,1)S(1)} %get-tuple-element.1116), channel_id=1, source_target_pairs={{0,8},{8,16},{16,24},{24,32},{32,40},{40,48},{48,56},{56,64},{64,7... | collective-permute-start | bytes 393224 | tf_op jit(solution)/shard_map/while/body/eval_jaxpr/ppermute | solution.py:27
  1256.5 8.9 all-to-all-start.1
  1265.4 8.9 all-to-all-start.2
  1282.7 8.9 all-to-all-start.3
  1312.0 15.3 collective-permute-start.2
  1346.3 8.9 all-to-all-start.1
  1401.8 15.3 collective-permute-start.2
  1436.0 8.9 all-to-all-start.1
  1491.5 14.8 collective-permute-start.2
  1525.2 8.9 all-to-all-start.1
  (219 other events, 2274.6 us)
